TPU v7x, 32 devices: a whole 2x2x4 slice. The times are simulated.
32 devices in a mesh: layer: 4 (over y, x), energy: 8 (over z, core).
Axes of the slice: x: 2, y: 2, z: 4, core: 2. Of those that a mesh axis runs over, the one named last changes fastest.
Arguments:
- onsite: float32 [4, 256], P('layer'), may hold values from -1 to 1
- broadening: float32 [4, 256], P('layer'), may hold values from 1 to 2
- hamiltonian: float32 [4, 2, 256, 256], P('layer'), may hold values from -0.078125 to 0.078125
- coupling: float32 [4, 2, 256, 256], P('layer'), may hold values from -0.21875 to 0.21875
- coupling_mask: int32 [4, 256, 256], P('layer'), may hold values 0 or 1
- prior_sigma: float32 [4, 32, 2, 256, 256], P('layer', 'energy'), may hold values from -0.4 to 0.4, as said below
- kernel_weights: float32 [8], replicated, may hold values from 0.1 to 0.6
- kernel_offsets: int32 [8], replicated, may hold values from -7 to 7
Outputs:
- self_energy: float32 [4, 32, 2, 256, 256], P('layer', 'energy')
Inputs may be any that keep to these rules, and one draw needn't show every extreme that they name: `prior_sigma`: real and imaginary parts of the blocks.
All inputs are finite; a program needn't handle non-finite values. No bound on the sum of `coupling_mask` on one device may be relied on, other than what follows from the above.
Results may differ from a plain program's by a relative error of at most 0.0001.
Values sent between devices are 32-bit elements; how exact they have to be, the bound alone decides.
No kernel may reach another device: no remote copies, remote signals or barrier semaphores. Data moves between devices by JAX's collectives and lax.ppermute only.
A program may use at most 128 MiB of HBM per device.

v0:
```python
import jax
import jax.numpy as jnp
from jax import lax
from jax.sharding import PartitionSpec as P

NS_ITERS = 3
exact_mode = lax.Precision.HIGHEST


def matmul_high(first_op, second_op):
    return jnp.matmul(first_op, second_op, precision=exact_mode)


def complex_product(first_op, second_op):
    first_real = first_op[..., 0, :, :]
    first_imag = first_op[..., 1, :, :]
    second_real = second_op[..., 0, :, :]
    second_imag = second_op[..., 1, :, :]
    real_part = matmul_high(first_real, second_real) - matmul_high(first_imag, second_imag)
    imag_part = matmul_high(first_real, second_imag) + matmul_high(first_imag, second_real)
    return jnp.stack([real_part, imag_part], axis=-3)


def adjoint(matrix):
    return jnp.stack(
        [jnp.swapaxes(matrix[..., 0, :, :], -1, -2), -jnp.swapaxes(matrix[..., 1, :, :], -1, -2)],
        axis=-3,
    )


def lead_block(batch_size, orbitals):
    identity = jnp.eye(orbitals, dtype=jnp.float32)
    single = jnp.stack([jnp.zeros_like(identity), -0.5 * identity])
    return jnp.broadcast_to(single, (batch_size, 2, orbitals, orbitals))


def energy_levels(positions, grid_size):
    return -1.0 + 2.0 * (positions.astype(jnp.float32) + 0.5) / grid_size


def solve_layer(
    levels, onsite_row, damping_row, hamilton, coupler, pattern, previous, incoming, sweeps
):
    orbitals = hamilton.shape[-1]
    identity = jnp.eye(orbitals, dtype=jnp.float32)
    hermitian = 0.5 * (hamilton + adjoint(hamilton))
    masked = coupler * pattern[None]
    contact = complex_product(complex_product(masked[None], incoming), adjoint(masked)[None])
    real_diag = levels[:, None] - onsite_row[None, :]
    imag_diag = damping_row[None, :]
    shifted = jnp.stack([real_diag, imag_diag], axis=1)[..., None, :] * identity
    system = shifted - hermitian[None] - contact - previous
    diag_real = jnp.diagonal(system[:, 0], axis1=-2, axis2=-1)
    diag_imag = jnp.diagonal(system[:, 1], axis1=-2, axis2=-1)
    modulus = diag_real * diag_real + diag_imag * diag_imag
    inverse = (
        jnp.stack([diag_real / modulus, -diag_imag / modulus], axis=1)[..., None, :] * identity
    )
    for sweep_no in range(sweeps):
        residue = complex_product(system, inverse)
        inverse = 2.0 * inverse - complex_product(inverse, residue)
    return inverse


def kernel_columns(weights, offsets, row_count, column_energy):
    row_idx = jnp.arange(row_count, dtype=jnp.int32)
    matches = column_energy[None, None, :] == row_idx[None, :, None] + offsets[:, None, None]
    return jnp.sum(jnp.where(matches, weights[:, None, None], jnp.float32(0.0)), axis=0)


def solve_all_layers(gathered, previous, levels_now, orbitals, layer_count):
    incoming = lead_block(levels_now.shape[0], orbitals)
    stacked = []
    for layer_no in range(layer_count):
        incoming = solve_layer(
            levels_now,
            gathered[0][layer_no],
            gathered[1][layer_no],
            gathered[2][layer_no],
            gathered[3][layer_no],
            gathered[4][layer_no],
            previous[layer_no],
            incoming,
            NS_ITERS,
        )
        stacked.append(incoming)
    return stacked


def local(
    onsite,
    broadening,
    hamiltonian,
    coupling,
    coupling_mask,
    prior_sigma,
    kernel_weights,
    kernel_offsets,
):
    layer_count = lax.axis_size("layer")
    group_count = lax.axis_size("energy")
    per_device = prior_sigma.shape[1]
    orbitals = prior_sigma.shape[-1]
    grid_size = per_device * group_count
    sub_count = per_device // layer_count
    first_level = lax.axis_index("energy") * per_device
    own_levels = energy_levels(first_level + jnp.arange(per_device, dtype=jnp.int32), grid_size)
    gathered = (
        lax.all_gather(onsite, "layer", axis=0, tiled=True),
        lax.all_gather(broadening, "layer", axis=0, tiled=True),
        lax.all_gather(hamiltonian, "layer", axis=0, tiled=True),
        lax.all_gather(coupling, "layer", axis=0, tiled=True),
        lax.all_gather(coupling_mask.astype(jnp.float32), "layer", axis=0, tiled=True),
    )
    previous = lax.all_to_all(prior_sigma, "layer", split_axis=1, concat_axis=0, tiled=True)
    levels_now = lax.dynamic_slice_in_dim(
        own_levels, lax.axis_index("layer") * sub_count, sub_count, 0
    )
    stacked = solve_all_layers(gathered, previous, levels_now, orbitals, layer_count)
    joined = jnp.concatenate(stacked, axis=2)
    arrived = lax.all_to_all(joined, ("layer", "energy"), split_axis=2, concat_axis=0, tiled=True)
    slot = jnp.arange(arrived.shape[0], dtype=jnp.int32)
    sender_layer = slot // (group_count * sub_count)
    sender_group = slot // sub_count % group_count
    column_energy = sender_group * per_device + sender_layer * sub_count + slot % sub_count
    kernel = kernel_columns(kernel_weights, kernel_offsets, grid_size, column_energy)
    blended = jnp.einsum("fe,epij->fpij", kernel, arrived, precision=exact_mode)
    scattering = lax.all_to_all(blended, "energy", split_axis=0, concat_axis=2, tiled=True)
    return scattering[None]


def solution(mesh):
    placed = (
        P("layer", None),
        P("layer", None),
        P("layer", None, None, None),
        P("layer", None, None, None),
        P("layer", None, None),
        P("layer", "energy", None, None, None),
        P(),
        P(),
    )
    return jax.shard_map(
        local,
        mesh=mesh,
        in_specs=placed,
        out_specs=P("layer", "energy", None, None, None),
        check_vma=False,
    )
```

profile of v0, /device:TPU:0, one launch (start us, length us, event | category | flops | bytes accessed | tf_op | source)
XLA Modules:
  0.0 352.6 jit_solution(5748276882402703983)
XLA Ops:
  6.5 1.7 convert_element_type.33
  9.7 5.2 %all-to-all-start = ((f32[1,4,2,256,256]{4,3,2,0,1:T(8,128)}), f32[1,4,2,256,256]{4,3,2,0,1:T(8,128)}, u32[]{:S(2)}, u32[]{:S(2)}) async-start(f32[1,4,2,256,256]{4,3,2,0,1:T(8,128)} %bitcast.628), calls=%async_computation | async-start | bytes 4194304 | tf_op jit(solution)/shard_map/all_to_all | solution.py:115
  15.5 30.2 %all-gather = f32[4,1,256]{2,1,0:T(1,128)S(1)} all-gather(f32[1,1,256]{2,1,0:T(1,128)S(1)} %bitcast.645), channel_id=1, replica_groups=mesh['layer'=4,'energy'=8] {'layer'}, dimensions={0}, use_global_device_ids=true | all-gather | bytes 5120 | tf_op jit(solution)/shard_map/all_gather | solution.py:109
  45.7 8.6 %all-gather.1 = f32[4,1,256]{2,1,0:T(1,128)S(1)} all-gather(f32[1,1,256]{2,1,0:T(1,128)S(1)} %bitcast.646), channel_id=1, replica_groups=mesh['layer'=4,'energy'=8] {'layer'}, dimensions={0}, use_global_device_ids=true | all-gather | bytes 5120 | tf_op jit(solution)/shard_map/all_gather | solution.py:110
  55.1 1.3 slice_bitcast_fusion.67
  56.4 30.5 %all-gather.8.cloned.1.call-done = f32[4,2,256,256]{3,2,1,0:T(8,128)} async-done(((f32[1,2,256,256]{3,2,1,0:T(8,128)}), f32[4,2,256,256]{3,2,1,0:T(8,128)}) %all-gather.8.cloned.1.call-update) | async-done | bytes 2097168 | tf_op jit(solution)/shard_map/all_gather | solution.py:112
  86.9 2.8 slice_multiply_fusion.3
  89.7 1.1 fusion.58
  90.8 1.1 fusion.57
  91.9 32.1 %all-gather.6.cloned.1.call-done = f32[4,2,256,256]{3,2,1,0:T(8,128)} async-done(((f32[1,2,256,256]{3,2,1,0:T(8,128)}), f32[4,2,256,256]{3,2,1,0:T(8,128)}) %all-gather.6.cloned.1.call-update) | async-done | bytes 2097168 | tf_op jit(solution)/shard_map/all_gather | solution.py:111
  123.9 2.8 fusion.132
  126.8 1.8 copy.76
  128.6 1.8 copy.75
  130.3 2.5 bitcast_multiply_fusion
  132.8 0.9 slice_bitcast_fusion.46
  135.0 1.1 fusion.34
  136.5 1.1 fusion.33
  137.7 1.4 fusion.47
  139.1 2.3 gather_fusion.1
  141.5 2.6 gather_fusion
  156.3 1.1 fusion.26
  157.4 1.5 fusion.25
  159.8 1.7 negate_bitcast_fusion.2
  162.3 1.5 fusion.43
  163.9 0.9 slice_bitcast_fusion.43
  164.7 2.6 gather_fusion.3
  167.3 2.6 gather_fusion.2
  181.0 0.9 slice_bitcast_fusion.14
  183.2 1.1 fusion.18
  184.3 1.1 fusion.17
  185.4 0.9 copy.80
  186.2 1.7 negate_bitcast_fusion.1
  188.8 1.5 fusion.39
  191.1 2.6 gather_fusion.5
  193.7 2.6 gather_fusion.4
  208.7 1.1 fusion.10
  209.9 1.1 fusion.9
  211.8 1.7 negate_bitcast_fusion
  214.3 1.5 fusion.35
  215.9 2.3 gather_fusion.7
  218.3 2.3 gather_fusion.6
  230.7 2.9 copy.67
  233.6 4.8 %all-to-all-start.1 = ((f32[1,2,1024,256]{3,1,0,2:T(2,128)}), f32[1,2,1024,256]{3,1,0,2:T(2,128)S(1)}, u32[]{:S(2)}, u32[]{:S(2)}) async-start(f32[1,2,1024,256]{3,1,0,2:T(2,128)} %copy.67), calls=%async_computation.1 | async-start | bytes 4194304 | tf_op jit(solution)/shard_map/all_to_all | solution.py:121
  238.7 49.8 %all-to-all-done.1 = f32[1,2,1024,256]{3,1,0,2:T(2,128)S(1)} async-done(((f32[1,2,1024,256]{3,1,0,2:T(2,128)}), f32[1,2,1024,256]{3,1,0,2:T(2,128)S(1)}, u32[]{:S(2)}, u32[]{:S(2)}) %all-to-all-start.1) | async-done | bytes 2097184 | tf_op jit(solution)/shard_map/all_to_all | solution.py:121
  288.5 3.0 fusion
  291.5 1.2 copy.70
  292.7 51.5 %all_to_all.45 = f32[32,2,32,256]{3,2,1,0:T(8,128)S(1)} all-to-all(f32[32,2,32,256]{3,2,1,0:T(8,128)S(1)} %copy.70), channel_id=1, replica_groups=mesh['layer'=4,'energy'=8] {'energy'}, dimensions={0} | all-to-all | bytes 4194304 | tf_op jit(solution)/shard_map/all_to_all | solution.py:128
  344.2 1.5 copy.71
  (247 shorter events, 55.7 us)
Async XLA Ops:
  6.5 48.5 %all-gather.10.cloned.1.call-start = ((), (), s32[]{:S(2)}) async-start(), calls=%async_computation.5 | async-start | bytes 1310720 | tf_op jit(solution)/shard_map/all_gather | solution.py:113
  8.2 78.6 %all-gather.8.cloned.1.call-start = ((), (), s32[]{:S(2)}) async-start(), calls=%async_computation.4 | async-start | bytes 2621440 | tf_op jit(solution)/shard_map/all_gather | solution.py:112
  9.0 115.0 %all-gather.6.cloned.1.call-start = ((), (), s32[]{:S(2)}) async-start(), calls=%async_computation.3 | async-start | bytes 2621440 | tf_op jit(solution)/shard_map/all_gather | solution.py:111
  9.7 5.8 %copy-start.29 = (f32[1,256]{1,0:T(1,128)S(1)}, f32[1,256]{1,0:T(1,128)}, u32[]{:S(2)}) copy-start(f32[1,256]{1,0:T(1,128)} %param.8) | copy-start | bytes 3076
  9.7 36.0 %copy-start.30 = (f32[1,256]{1,0:T(1,128)S(1)}, f32[1,256]{1,0:T(1,128)}, u32[]{:S(2)}) copy-start(f32[1,256]{1,0:T(1,128)} %param.9) | copy-start | bytes 3076
  9.7 128.0 %all-to-all-start = ((f32[1,4,2,256,256]{4,3,2,0,1:T(8,128)}), f32[1,4,2,256,256]{4,3,2,0,1:T(8,128)}, u32[]{:S(2)}, u32[]{:S(2)}) async-start(f32[1,4,2,256,256]{4,3,2,0,1:T(8,128)} %bitcast.628), calls=%async_computation | async-start | bytes 4194304 | tf_op jit(solution)/shard_map/all_to_all | solution.py:115
  56.3 33.3 %copy-start.9 = (f32[256,256]{1,0:T(8,128)}, f32[256,256]{1,0:T(8,128)S(1)}, u32[]{:S(2)}) copy-start(f32[256,256]{1,0:T(8,128)S(1)} %get-tuple-element.21) | copy-start | bytes 786436
  56.4 33.3 %copy-start.10 = (f32[256,256]{1,0:T(8,128)}, f32[256,256]{1,0:T(8,128)S(1)}, u32[]{:S(2)}) copy-start(f32[256,256]{1,0:T(8,128)S(1)} %get-tuple-element.22) | copy-start | bytes 786436
  56.4 33.3 %copy-start.11 = (f32[256,256]{1,0:T(8,128)}, f32[256,256]{1,0:T(8,128)S(1)}, u32[]{:S(2)}) copy-start(f32[256,256]{1,0:T(8,128)S(1)} %get-tuple-element.23) | copy-start | bytes 786436
  56.4 33.3 %copy-start.12 = (f32[256,256]{1,0:T(8,128)}, f32[256,256]{1,0:T(8,128)S(1)}, u32[]{:S(2)}) copy-start(f32[256,256]{1,0:T(8,128)S(1)} %get-tuple-element.24) | copy-start | bytes 786436
  91.9 38.5 %copy-start.1 = (f32[4,2,256,256]{3,2,1,0:T(8,128)S(1)}, f32[4,2,256,256]{3,2,1,0:T(8,128)}, u32[]{:S(2)}) copy-start(f32[4,2,256,256]{3,2,1,0:T(8,128)} %all-gather.8.cloned.1.call-done) | copy-start | bytes 6291460
  132.8 0.9 copy-start.24
  132.8 1.8 copy-start.22
  134.6 3.1 copy-start.23
  134.6 3.1 copy-start
  135.0 2.8 copy-start.21
  152.8 1.0 copy-start.8
  153.6 1.4 copy-start.25
  153.6 1.4 copy-start.26
  155.5 3.5 copy-start.20
  155.9 5.6 %copy-start.19 = (f32[1,1,256,256]{3,2,1,0:T(8,128)S(1)}, f32[1,1,256,256]{3,2,1,0:T(8,128)}, u32[]{:S(2)}) copy-start(f32[1,1,256,256]{3,2,1,0:T(8,128)} %get-tuple-element.18) | copy-start | bytes 786436
  178.6 1.0 copy-start.7
  179.4 1.6 copy-start.13
  179.4 1.6 copy-start.14
  179.5 3.2 copy-start.2
  182.3 3.1 copy-start.18
  182.8 5.2 %copy-start.17 = (f32[1,1,256,256]{3,2,1,0:T(8,128)S(1)}, f32[1,1,256,256]{3,2,1,0:T(8,128)}, u32[]{:S(2)}) copy-start(f32[1,1,256,256]{3,2,1,0:T(8,128)} %get-tuple-element.16) | copy-start | bytes 786436
  205.2 1.0 copy-start.6
  206.0 1.4 copy-start.27
  206.0 1.4 copy-start.28
  206.1 2.2 copy-start.4
  207.9 3.1 copy-start.16
  208.3 5.2 %copy-start.15 = (f32[1,1,256,256]{3,2,1,0:T(8,128)S(1)}, f32[1,1,256,256]{3,2,1,0:T(8,128)}, u32[]{:S(2)}) copy-start(f32[1,1,256,256]{3,2,1,0:T(8,128)} %get-tuple-element.14) | copy-start | bytes 786436
  229.3 1.0 copy-start.3
  229.3 1.2 copy-start.5
  233.6 4.9 %copy-start.31 = (s32[8]{0:T(128)S(1)}, s32[8]{0:T(128)}, u32[]{:S(2)}) copy-start(s32[8]{0:T(128)} %param.15) | copy-start | bytes 100
  233.6 5.0 %copy-start.32 = (f32[8]{0:T(128)S(1)}, f32[8]{0:T(128)}, u32[]{:S(2)}) copy-start(f32[8]{0:T(128)} %param.14) | copy-start | bytes 100
  233.6 54.9 %all-to-all-start.1 = ((f32[1,2,1024,256]{3,1,0,2:T(2,128)}), f32[1,2,1024,256]{3,1,0,2:T(2,128)S(1)}, u32[]{:S(2)}, u32[]{:S(2)}) async-start(f32[1,2,1024,256]{3,1,0,2:T(2,128)} %copy.67), calls=%async_computation.1 | async-start | bytes 4194304 | tf_op jit(solution)/shard_map/all_to_all | solution.py:121
Sparse Core Ops, SparseCore 0:
  9.2 40.0 all-gather.9
  51.1 35.6 all-gather.7
  88.7 35.1 all-gather.5
where the time goes:
time: 358 us; the launch traced here: 353 us
  waiting for transfers between devices  114 us (32%)
  blocking collectives  90.2 us (25%)
  matrix products  59.9 us (17%)
  local copies, waits for them, and re-layouts  41.3 us (12%)
  other arithmetic  22.2 us (6%)
  between operations  15.2 us (4%)
  starting transfers between devices  10.1 us (3%)
    dot_general x128, matrix products, matmul_high(): return jnp.matmul(first_op, second_op, precision=exact_mode)  56.9 us
    all_to_all x1, blocking collectives, local(): lax.all_to_all(blended, 'energy', split_axis=0, concat_axis=2, tiled=True)  51.5 us
    all_to_all x1, waiting for transfers between devices, local(): lax.all_to_all(joined, ('layer', 'energy'), split_axis=2, concat_axis=0,...  49.8 us
    all_gather x1, waiting for transfers between devices, local(): lax.all_gather(hamiltonian, 'layer', axis=0, tiled=True)  32.1 us
    all_gather x1, waiting for transfers between devices, local(): lax.all_gather(coupling, 'layer', axis=0, tiled=True)  30.5 us
    all_gather x1, blocking collectives, local(): lax.all_gather(onsite, 'layer', axis=0, tiled=True)  30.2 us
    gather x4, local copies, waits for them, and re-layouts, solve_layer(): diag_real = jnp.diagonal(system[:, 0], axis1=-2, axis2=-1)  10 us
    gather x4, local copies, waits for them, and re-layouts, solve_layer(): diag_imag = jnp.diagonal(system[:, 1], axis1=-2, axis2=-1)  9.82 us
  transfers between devices with their start and end apart: 5, of which 3 were waited for; matrix products, arithmetic and copies ran while one was open for 6% of the time, Pallas kernels for 0%

commit v1 on v0

--- a/solution.py
+++ b/solution.py
@@ -118,7 +118,15 @@
     )
     stacked = solve_all_layers(gathered, previous, levels_now, orbitals, layer_count)
     joined = jnp.concatenate(stacked, axis=2)
-    arrived = lax.all_to_all(joined, ("layer", "energy"), split_axis=2, concat_axis=0, tiled=True)
+    arrived = jnp.concatenate(
+        lax.all_to_all(
+            jnp.stack(jnp.split(joined, lax.axis_size(("layer", "energy")), axis=2)),
+            ("layer", "energy"),
+            0,
+            0,
+        ),
+        axis=0,
+    )
     slot = jnp.arange(arrived.shape[0], dtype=jnp.int32)
     sender_layer = slot // (group_count * sub_count)
     sender_group = slot // sub_count % group_count

time: 358 us -> 376 us (1.050)
  local copies, waits for them, and re-layouts: 41.3 us -> 58.6 us
    unnamed x74 -> x105, local copies, waits for them, and re-layouts: 9.31 us -> 28.7 us
where the time goes in v1:
time: 376 us; the launch traced here: 370 us
  waiting for transfers between devices  114 us (30%)
  blocking collectives  90.2 us (24%)
  matrix products  59.9 us (16%)
  local copies, waits for them, and re-layouts  58.6 us (16%)
  other arithmetic  22 us (6%)
  between operations  15.3 us (4%)
  starting transfers between devices  10.2 us (3%)
    dot_general x128, matrix products, matmul_high(): return jnp.matmul(first_op, second_op, precision=exact_mode)  56.9 us
    all_to_all x1, blocking collectives, local(): lax.all_to_all(blended, 'energy', split_axis=0, concat_axis=2, tiled=True)  51.5 us
    all_to_all x1, waiting for transfers between devices, local(): lax.all_to_all(jnp.stack(jnp.split(joined, lax.axis_size(('layer', 'energ...  49.8 us
    all_gather x1, waiting for transfers between devices, local(): lax.all_gather(hamiltonian, 'layer', axis=0, tiled=True)  32.1 us
    all_gather x1, waiting for transfers between devices, local(): lax.all_gather(coupling, 'layer', axis=0, tiled=True)  30.5 us
    all_gather x1, blocking collectives, local(): lax.all_gather(onsite, 'layer', axis=0, tiled=True)  30.2 us
    unnamed x105, local copies, waits for them, and re-layouts  28.7 us
    gather x4, local copies, waits for them, and re-layouts, solve_layer(): diag_real = jnp.diagonal(system[:, 0], axis1=-2, axis2=-1)  10.3 us
  transfers between devices with their start and end apart: 5, of which 3 were waited for; matrix products, arithmetic and copies ran while one was open for 6% of the time, Pallas kernels for 0%

profile of v1, /device:TPU:0, one launch (start us, length us, event | category | flops | bytes accessed | tf_op | source)
XLA Modules:
  0.0 370.0 jit_solution(8681470914019702055)
XLA Ops:
  6.5 1.7 convert_element_type.33
  9.7 5.2 %all-to-all-start = ((f32[1,4,2,256,256]{4,3,2,0,1:T(8,128)}), f32[1,4,2,256,256]{4,3,2,0,1:T(8,128)}, u32[]{:S(2)}, u32[]{:S(2)}) async-start(f32[1,4,2,256,256]{4,3,2,0,1:T(8,128)} %bitcast.751), calls=%async_computation | async-start | bytes 4194304 | tf_op jit(solution)/shard_map/all_to_all | solution.py:115
  15.5 30.2 %all-gather = f32[4,1,256]{2,1,0:T(1,128)S(1)} all-gather(f32[1,1,256]{2,1,0:T(1,128)S(1)} %bitcast.768), channel_id=1, replica_groups=mesh['layer'=4,'energy'=8] {'layer'}, dimensions={0}, use_global_device_ids=true | all-gather | bytes 5120 | tf_op jit(solution)/shard_map/all_gather | solution.py:109
  45.7 8.6 %all-gather.1 = f32[4,1,256]{2,1,0:T(1,128)S(1)} all-gather(f32[1,1,256]{2,1,0:T(1,128)S(1)} %bitcast.769), channel_id=1, replica_groups=mesh['layer'=4,'energy'=8] {'layer'}, dimensions={0}, use_global_device_ids=true | all-gather | bytes 5120 | tf_op jit(solution)/shard_map/all_gather | solution.py:110
  55.1 1.3 slice_bitcast_fusion.19
  56.4 30.5 %all-gather.8.cloned.1.call-done = f32[4,2,256,256]{3,2,1,0:T(8,128)} async-done(((f32[1,2,256,256]{3,2,1,0:T(8,128)}), f32[4,2,256,256]{3,2,1,0:T(8,128)}) %all-gather.8.cloned.1.call-update) | async-done | bytes 2097168 | tf_op jit(solution)/shard_map/all_gather | solution.py:112
  86.9 2.8 slice_multiply_fusion
  89.7 1.1 fusion.57
  90.8 1.1 fusion.56
  91.9 32.1 %all-gather.6.cloned.1.call-done = f32[4,2,256,256]{3,2,1,0:T(8,128)} async-done(((f32[1,2,256,256]{3,2,1,0:T(8,128)}), f32[4,2,256,256]{3,2,1,0:T(8,128)}) %all-gather.6.cloned.1.call-update) | async-done | bytes 2097168 | tf_op jit(solution)/shard_map/all_gather | solution.py:111
  123.9 2.9 fusion.131
  126.8 1.8 copy.55
  128.6 1.8 copy.54
  130.4 2.5 bitcast_multiply_fusion
  132.9 0.9 slice_bitcast_fusion.46
  135.0 1.1 fusion.33
  136.6 1.1 fusion.32
  137.8 1.4 fusion.46
  139.2 2.3 gather_fusion.1
  141.6 2.6 gather_fusion
  156.4 1.1 fusion.25
  157.5 1.5 fusion.24
  159.9 1.7 negate_bitcast_fusion.2
  161.5 0.8 copy.56
  162.4 1.5 fusion.42
  163.9 0.9 slice_bitcast_fusion.43
  164.8 2.6 gather_fusion.3
  167.3 2.6 gather_fusion.2
  181.0 0.9 slice_bitcast_fusion.14
  183.2 1.1 fusion.17
  184.3 1.1 fusion.16
  185.4 0.9 copy.59
  186.3 1.7 negate_bitcast_fusion.1
  188.8 1.5 fusion.38
  191.1 2.6 gather_fusion.5
  193.7 2.6 gather_fusion.4
  208.8 1.1 fusion.9
  209.9 1.1 fusion.8
  211.9 1.7 negate_bitcast_fusion
  214.4 1.5 fusion.34
  215.9 2.3 gather_fusion.7
  218.3 2.6 gather_fusion.6
  250.9 4.9 %all-to-all-start.1 = ((f32[32,1,2,32,256]{4,3,2,1,0:T(8,128)}), f32[32,1,2,32,256]{4,3,2,1,0:T(8,128)S(1)}, u32[]{:S(2)}, u32[]{:S(2)}) async-start(f32[32,1,2,32,256]{4,3,2,1,0:T(8,128)} %constant_dynamic-update-slice_fusion), calls=%async_computation.1 | async-start | bytes 4194304 | tf_op jit(solution)/shard_map/all_to_all | solution.py:122
  256.0 49.8 %all-to-all-done.1 = f32[32,1,2,32,256]{4,3,2,1,0:T(8,128)S(1)} async-done(((f32[32,1,2,32,256]{4,3,2,1,0:T(8,128)}), f32[32,1,2,32,256]{4,3,2,1,0:T(8,128)S(1)}, u32[]{:S(2)}, u32[]{:S(2)}) %all-to-all-start.1) | async-done | bytes 2097184 | tf_op jit(solution)/shard_map/all_to_all | solution.py:122
  305.8 3.0 fusion
  308.8 1.2 copy.51
  310.0 51.5 %all_to_all.32 = f32[32,2,32,256]{3,2,1,0:T(8,128)S(1)} all-to-all(f32[32,2,32,256]{3,2,1,0:T(8,128)S(1)} %copy.51), channel_id=1, replica_groups=mesh['layer'=4,'energy'=8] {'energy'}, dimensions={0} | all-to-all | bytes 4194304 | tf_op jit(solution)/shard_map/all_to_all | solution.py:136
  361.5 1.5 copy.52
  (277 shorter events, 74.7 us)
Async XLA Ops:
  6.5 48.5 %all-gather.10.cloned.1.call-start = ((), (), s32[]{:S(2)}) async-start(), calls=%async_computation.5 | async-start | bytes 1310720 | tf_op jit(solution)/shard_map/all_gather | solution.py:113
  8.2 78.6 %all-gather.8.cloned.1.call-start = ((), (), s32[]{:S(2)}) async-start(), calls=%async_computation.4 | async-start | bytes 2621440 | tf_op jit(solution)/shard_map/all_gather | solution.py:112
  9.0 115.0 %all-gather.6.cloned.1.call-start = ((), (), s32[]{:S(2)}) async-start(), calls=%async_computation.3 | async-start | bytes 2621440 | tf_op jit(solution)/shard_map/all_gather | solution.py:111
  9.7 5.8 %copy-start.29 = (f32[1,256]{1,0:T(1,128)S(1)}, f32[1,256]{1,0:T(1,128)}, u32[]{:S(2)}) copy-start(f32[1,256]{1,0:T(1,128)} %param.8) | copy-start | bytes 3076
  9.7 36.0 %copy-start.30 = (f32[1,256]{1,0:T(1,128)S(1)}, f32[1,256]{1,0:T(1,128)}, u32[]{:S(2)}) copy-start(f32[1,256]{1,0:T(1,128)} %param.9) | copy-start | bytes 3076
  9.7 128.0 %all-to-all-start = ((f32[1,4,2,256,256]{4,3,2,0,1:T(8,128)}), f32[1,4,2,256,256]{4,3,2,0,1:T(8,128)}, u32[]{:S(2)}, u32[]{:S(2)}) async-start(f32[1,4,2,256,256]{4,3,2,0,1:T(8,128)} %bitcast.751), calls=%async_computation | async-start | bytes 4194304 | tf_op jit(solution)/shard_map/all_to_all | solution.py:115
  56.3 33.3 %copy-start.9 = (f32[256,256]{1,0:T(8,128)}, f32[256,256]{1,0:T(8,128)S(1)}, u32[]{:S(2)}) copy-start(f32[256,256]{1,0:T(8,128)S(1)} %get-tuple-element.21) | copy-start | bytes 786436
  56.4 33.3 %copy-start.10 = (f32[256,256]{1,0:T(8,128)}, f32[256,256]{1,0:T(8,128)S(1)}, u32[]{:S(2)}) copy-start(f32[256,256]{1,0:T(8,128)S(1)} %get-tuple-element.22) | copy-start | bytes 786436
  56.4 33.3 %copy-start.11 = (f32[256,256]{1,0:T(8,128)}, f32[256,256]{1,0:T(8,128)S(1)}, u32[]{:S(2)}) copy-start(f32[256,256]{1,0:T(8,128)S(1)} %get-tuple-element.23) | copy-start | bytes 786436
  56.4 33.3 %copy-start.12 = (f32[256,256]{1,0:T(8,128)}, f32[256,256]{1,0:T(8,128)S(1)}, u32[]{:S(2)}) copy-start(f32[256,256]{1,0:T(8,128)S(1)} %get-tuple-element.24) | copy-start | bytes 786436
  91.9 38.5 %copy-start.1 = (f32[4,2,256,256]{3,2,1,0:T(8,128)S(1)}, f32[4,2,256,256]{3,2,1,0:T(8,128)}, u32[]{:S(2)}) copy-start(f32[4,2,256,256]{3,2,1,0:T(8,128)} %all-gather.8.cloned.1.call-done) | copy-start | bytes 6291460
  132.9 0.9 copy-start.24
  132.9 1.8 copy-start.22
  134.6 3.1 copy-start.23
  134.6 3.1 copy-start
  135.0 2.7 copy-start.21
  152.8 1.0 copy-start.8
  153.6 1.4 copy-start.25
  153.6 1.4 copy-start.26
  155.5 3.5 copy-start.20
  156.0 5.6 %copy-start.19 = (f32[1,1,256,256]{3,2,1,0:T(8,128)S(1)}, f32[1,1,256,256]{3,2,1,0:T(8,128)}, u32[]{:S(2)}) copy-start(f32[1,1,256,256]{3,2,1,0:T(8,128)} %get-tuple-element.17) | copy-start | bytes 786436
  178.6 1.0 copy-start.7
  179.4 1.6 copy-start.13
  179.4 1.6 copy-start.14
  179.6 3.2 copy-start.2
  182.4 3.1 copy-start.18
  182.8 5.2 %copy-start.17 = (f32[1,1,256,256]{3,2,1,0:T(8,128)S(1)}, f32[1,1,256,256]{3,2,1,0:T(8,128)}, u32[]{:S(2)}) copy-start(f32[1,1,256,256]{3,2,1,0:T(8,128)} %get-tuple-element.15) | copy-start | bytes 786436
  205.3 1.0 copy-start.6
  206.0 1.4 copy-start.27
  206.0 1.4 copy-start.28
  206.2 2.2 copy-start.4
  207.9 3.1 copy-start.16
  208.4 5.2 %copy-start.15 = (f32[1,1,256,256]{3,2,1,0:T(8,128)S(1)}, f32[1,1,256,256]{3,2,1,0:T(8,128)}, u32[]{:S(2)}) copy-start(f32[1,1,256,256]{3,2,1,0:T(8,128)} %get-tuple-element.13) | copy-start | bytes 786436
  229.9 5.6 %copy-start.3 = (f32[1,2,256,256]{3,2,1,0:T(8,128)S(1)}, f32[1,2,256,256]{3,2,1,0:T(8,128)}, u32[]{:S(2)}) copy-start(f32[1,2,256,256]{3,2,1,0:T(8,128)} %copy-done.2) | copy-start | bytes 1572868
  230.3 10.3 %copy-start.5 = (f32[1,2,256,256]{3,2,1,0:T(8,128)S(1)}, f32[1,2,256,256]{3,2,1,0:T(8,128)}, u32[]{:S(2)}) copy-start(f32[1,2,256,256]{3,2,1,0:T(8,128)} %copy-done.4) | copy-start | bytes 1572868
  250.9 4.9 %copy-start.31 = (s32[8]{0:T(128)S(1)}, s32[8]{0:T(128)}, u32[]{:S(2)}) copy-start(s32[8]{0:T(128)} %param.15) | copy-start | bytes 100
  250.9 5.0 %copy-start.32 = (f32[8]{0:T(128)S(1)}, f32[8]{0:T(128)}, u32[]{:S(2)}) copy-start(f32[8]{0:T(128)} %param.14) | copy-start | bytes 100
  250.9 54.9 %all-to-all-start.1 = ((f32[32,1,2,32,256]{4,3,2,1,0:T(8,128)}), f32[32,1,2,32,256]{4,3,2,1,0:T(8,128)S(1)}, u32[]{:S(2)}, u32[]{:S(2)}) async-start(f32[32,1,2,32,256]{4,3,2,1,0:T(8,128)} %constant_dynamic-update-slice_fusion), calls=%async_computation.1 | async-start | bytes 4194304 | tf_op jit(solution)/shard_map/all_to_all | solution.py:122
Sparse Core Ops, SparseCore 0:
  9.2 40.0 all-gather.9
  51.1 35.6 all-gather.7
  88.7 35.1 all-gather.5
